TPU v7x, 256 devices: a whole 4x4x8 slice. The times are simulated.
256 devices in a mesh: dp: 32 (over z, y_hi, core), tensor: 8 (over x, y_lo).
Axes of the slice: x: 4, y: 4 (y_hi: 2, y_lo: 2; y = y_hi * 2 + y_lo), z: 8, core: 2. Of those that a mesh axis runs over, the one named last changes fastest.
Arguments:
- tokens: bfloat16 [128, 576, 1024], P('dp', 'tensor'), may hold values from -150 to 150
- cotangent: bfloat16 [128, 576, 1024], P('dp', 'tensor'), may hold values from -6 to 6
- dispatch_weight: bfloat16 [1024, 64], replicated, may hold values from -3 to 3
- w_in: bfloat16 [64, 1024, 4096], P('dp', None, 'tensor'), may hold values from -0.1875 to 0.1875
- w_out: bfloat16 [64, 4096, 1024], P('dp', 'tensor'), may hold values from -0.09375 to 0.09375
Outputs:
- grad_tokens: bfloat16 [128, 576, 1024], P('dp', 'tensor')
- grad_router: float32 [1024, 64], replicated
- grad_w_in: bfloat16 [64, 1024, 4096], P('dp', None, 'tensor')
- grad_w_out: bfloat16 [64, 4096, 1024], P('dp', 'tensor')
All inputs are finite; a program needn't handle non-finite values.
Results may differ from a plain program's by a relative error of at most 0.0079.
Values may be sent and summed in bfloat16 or wider, within the bound.
A program may use at most 64 MiB of HBM per device.

v0:
```python
import jax
import jax.numpy as jnp
from jax import lax
from jax.sharding import PartitionSpec as P


def split_up(x, dim, length):
    lengths = x.shape
    blocks = x.reshape(*lengths[:dim], length, lengths[dim] // length, *lengths[dim + 1 :])
    return jnp.moveaxis(blocks, dim, 0)


def summed_on_arrival(x, axis, dim):
    blocks = split_up(x, dim, lax.axis_size(axis))
    arrived = lax.all_to_all(blocks, axis, split_axis=0, concat_axis=0, tiled=True)
    return arrived.sum(axis=0)


def sent_to_all(x, axis):
    length = lax.axis_size(axis)
    return lax.all_to_all(jnp.broadcast_to(x[None], (length, *x.shape)), axis, 0, 0, tiled=True)


def laid_out(blocks, dim):
    lengths = list(blocks.shape[1:])
    lengths[dim] *= blocks.shape[0]
    return jnp.moveaxis(blocks, 0, dim).reshape(lengths)


def gathered_copies(x, axis, dim):
    blocks = sent_to_all(x, axis)
    return laid_out(blocks, dim)


def collected_together(x, axis):
    leaves = jax.tree.leaves(x)
    sequence = sorted(range(len(leaves)), key=lambda k: -leaves[k].size)
    width = (1, *leaves[sequence[0]].shape)[-1]
    lines = [
        jnp.pad(leaves[k].reshape(-1), (0, -leaves[k].size % width)).reshape(-1, width)
        for k in sequence
    ]
    both, at, found = (sent_to_all(jnp.concatenate(lines), axis), 0, {})
    for k, line in zip(sequence, lines):
        piece = both[:, at : at + len(line)].reshape(len(both), -1)
        found[k] = piece[:, : leaves[k].size].reshape(-1, *leaves[k].shape)
        at += len(line)
    numbers = iter(range(len(leaves)))
    return jax.tree.map(lambda _: found[next(numbers)], x)


def combined_pairwise(pieces, combine):
    while len(jax.tree.leaves(pieces)[0]) > 1:
        pieces = jax.vmap(combine)(
            *(jax.tree.map(lambda part: part[side::2], pieces) for side in (0, 1))
        )
    return jax.tree.map(lambda part: part[0], pieces)


def merged(x, axis, combine):
    pieces = collected_together(x, axis)
    return combined_pairwise(pieces, combine)


def over_copies(x, axis):
    return sent_to_all(x, axis).sum(axis=0)


def to_experts(partial_rows):
    shared_part = summed_on_arrival(partial_rows, "tensor", 2).astype(jnp.bfloat16)
    arrived = lax.all_to_all(shared_part, "dp", split_axis=1, concat_axis=0, tiled=True)
    result = gathered_copies(arrived, "tensor", 2)
    return result


def to_images(partial_rows):
    shared_part = summed_on_arrival(partial_rows, "tensor", 2).astype(jnp.bfloat16)
    arrived = lax.all_to_all(shared_part, "dp", split_axis=0, concat_axis=1, tiled=True)
    result = gathered_copies(arrived, "tensor", 2)
    return result


def join_stats(former, latter):
    biggest = jnp.maximum(former[0], latter[0])
    return (
        biggest,
        former[1] * jnp.exp(former[0] - biggest) + latter[1] * jnp.exp(latter[0] - biggest),
    )


def dispatch_softmax(logits):
    local_max = jnp.max(logits, axis=1)
    local_total = jnp.sum(jnp.exp(logits - local_max[:, None, :]), axis=1)
    global_max, totals = merged((local_max, local_total), "tensor", join_stats)
    exponent = jnp.exp(logits - global_max[:, None, :])
    return exponent / totals[:, None, :]


def on_device(tokens, cotangent, dispatch_weight, w_in, w_out):
    wide = jnp.float32
    logits = jnp.einsum("isd,de->ise", tokens, dispatch_weight, preferred_element_type=wide)
    dispatch = dispatch_softmax(logits)
    combine = jax.nn.softmax(logits, axis=2)
    dispatch_low = dispatch.astype(jnp.bfloat16)
    combine_low = combine.astype(jnp.bfloat16)
    slot_inputs = to_experts(
        jnp.einsum("ise,isd->ied", dispatch_low, tokens, preferred_element_type=wide)
    )
    pre_act = jnp.einsum("ied,edf->ief", slot_inputs, w_in, preferred_element_type=wide)
    hidden_act, gelu_back = jax.vjp(jax.nn.gelu, pre_act)
    hidden_low = hidden_act.astype(jnp.bfloat16)
    slot_outputs = to_images(
        jnp.einsum("ief,efd->ied", hidden_low, w_out, preferred_element_type=wide)
    )
    grad_combine = jnp.einsum("isd,ied->ise", cotangent, slot_outputs, preferred_element_type=wide)
    grad_slots_out = to_experts(
        jnp.einsum("ise,isd->ied", combine_low, cotangent, preferred_element_type=wide)
    )
    grad_hidden = jnp.einsum("ied,efd->ief", grad_slots_out, w_out, preferred_element_type=wide)
    grad_pre = gelu_back(grad_hidden)[0].astype(jnp.bfloat16)
    grad_w_out = jnp.einsum(
        "ief,ied->efd", hidden_low, grad_slots_out, preferred_element_type=wide
    ).astype(jnp.bfloat16)
    grad_w_in = jnp.einsum(
        "ied,ief->edf", slot_inputs, grad_pre, preferred_element_type=wide
    ).astype(jnp.bfloat16)
    grad_slots_in = to_images(
        jnp.einsum("ief,edf->ied", grad_pre, w_in, preferred_element_type=wide)
    )
    grad_dispatch = jnp.einsum("isd,ied->ise", tokens, grad_slots_in, preferred_element_type=wide)
    column_dot = over_copies(jnp.sum(grad_dispatch * dispatch, axis=1), "tensor")
    row_dot = jnp.sum(grad_combine * combine, axis=2, keepdims=True)
    grad_logits = (
        combine * (grad_combine - row_dot) + dispatch * (grad_dispatch - column_dot[:, None, :])
    ).astype(jnp.bfloat16)
    token_part = jnp.einsum(
        "ise,ied->isd", dispatch_low, grad_slots_in, preferred_element_type=wide
    )
    router_part = jnp.einsum(
        "ise,de->isd", grad_logits, dispatch_weight, preferred_element_type=wide
    )
    grad_tokens = (token_part + router_part).astype(jnp.bfloat16)
    local_router = jnp.einsum("isd,ise->de", tokens, grad_logits, preferred_element_type=wide)
    grad_router = lax.psum(local_router, ("dp", "tensor"))
    return (grad_tokens, grad_router, grad_w_in, grad_w_out)


def solution(mesh):
    return jax.shard_map(
        on_device,
        mesh=mesh,
        in_specs=(
            P("dp", "tensor", None),
            P("dp", "tensor", None),
            P(),
            P("dp", None, "tensor"),
            P("dp", "tensor", None),
        ),
        out_specs=(P("dp", "tensor", None), P(), P("dp", None, "tensor"), P("dp", "tensor", None)),
        check_vma=False,
    )
```

profile of v0, /device:TPU:2, one launch (start us, length us, event | category | flops | bytes accessed | tf_op | source)
XLA Modules:
  0.0 496.0 jit_solution(7292811887007530040)
XLA Ops:
  9.2 10.4 %all_to_all.110 = f32[8,1,512]{2,1,0:T(1,128)S(1)} all-to-all(f32[8,1,512]{2,1,0:T(1,128)S(1)} %reshape.63), channel_id=1, replica_groups=mesh['dp'=32,'tensor'=8] {'tensor'}, dimensions={0} | all-to-all | bytes 32768 | tf_op jit(solution)/shard_map/all_to_all | solution.py:21
  23.4 5.6 %all-to-all-start.4 = ((f32[8,4,64,128]{3,2,1,0:T(8,128)}), f32[8,4,64,128]{3,2,1,0:T(8,128)}, u32[]{:S(2)}, u32[]{:S(2)}) async-start(f32[8,4,64,128]{3,2,1,0:T(8,128)} %bitcast.137), calls=%async_computation.4 | async-start | bytes 2097152 | tf_op jit(solution)/shard_map/all_to_all | solution.py:15
  32.1 9.9 %all-to-all-done.4 = f32[8,4,64,128]{3,2,1,0:T(8,128)} async-done(((f32[8,4,64,128]{3,2,1,0:T(8,128)}), f32[8,4,64,128]{3,2,1,0:T(8,128)}, u32[]{:S(2)}, u32[]{:S(2)}) %all-to-all-start.4) | async-done | bytes 1048608 | tf_op jit(solution)/shard_map/all_to_all | solution.py:15
  42.1 4.9 all-to-all-start.1
  49.0 11.1 %all-to-all-done.1 = f32[8,4,64,128]{3,2,1,0:T(8,128)S(1)} async-done(((f32[8,4,64,128]{3,2,1,0:T(8,128)}), f32[8,4,64,128]{3,2,1,0:T(8,128)S(1)}, u32[]{:S(2)}, u32[]{:S(2)}) %all-to-all-start.1) | async-done | bytes 1048608 | tf_op jit(solution)/shard_map/all_to_all | solution.py:15
  60.1 11.2 %all-to-all-start.5 = ((bf16[4,64,128]{2,0,1:T(4,128)(2,1)}), bf16[4,64,128]{2,0,1:T(4,128)(2,1)S(1)}, u32[]{:S(2)}, u32[]{:S(2)}) async-start(bf16[4,64,128]{2,0,1:T(4,128)(2,1)} %copy.87), calls=%async_computation.5 | async-start | bytes 131072 | tf_op jit(solution)/shard_map/all_to_all | solution.py:71
  72.0 9.2 %all-to-all-done.5 = bf16[4,64,128]{2,0,1:T(4,128)(2,1)S(1)} async-done(((bf16[4,64,128]{2,0,1:T(4,128)(2,1)}), bf16[4,64,128]{2,0,1:T(4,128)(2,1)S(1)}, u32[]{:S(2)}, u32[]{:S(2)}) %all-to-all-start.5) | async-done | bytes 65568 | tf_op jit(solution)/shard_map/all_to_all | solution.py:71
  85.2 9.9 %all-to-all-done.2 = bf16[4,64,128]{2,0,1:T(4,128)(2,1)S(1)} async-done(((bf16[4,64,128]{2,0,1:T(4,128)(2,1)}), bf16[4,64,128]{2,0,1:T(4,128)(2,1)S(1)}, u32[]{:S(2)}, u32[]{:S(2)}) %all-to-all-start.2) | async-done | bytes 65568 | tf_op jit(solution)/shard_map/all_to_all | solution.py:71
  95.9 4.9 all-to-all-start.6
  100.9 8.5 %all-to-all-done.6 = bf16[8,128,2,128]{3,1,2,0:T(8,128)(2,1)S(1)} async-done(((bf16[8,128,2,128]{3,1,2,0:T(8,128)(2,1)}), bf16[8,128,2,128]{3,1,2,0:T(8,128)(2,1)S(1)}, u32[]{:S(2)}, u32[]{:S(2)}) %all-to-all-start.6) | async-done | bytes 524320 | tf_op jit(solution)/shard_map/all_to_all | solution.py:21
  110.3 5.5 %all-to-all-start.3 = ((bf16[8,128,2,128]{3,1,2,0:T(8,128)(2,1)}), bf16[8,128,2,128]{3,1,2,0:T(8,128)(2,1)}, u32[]{:S(2)}, u32[]{:S(2)}) async-start(bf16[8,128,2,128]{3,1,2,0:T(8,128)(2,1)} %broadcast_in_dim.22), calls=%async_computation.3 | async-start | bytes 1048576 | tf_op jit(solution)/shard_map/all_to_all | solution.py:21
  116.2 7.5 %all-to-all-done.3 = bf16[8,128,2,128]{3,1,2,0:T(8,128)(2,1)} async-done(((bf16[8,128,2,128]{3,1,2,0:T(8,128)(2,1)}), bf16[8,128,2,128]{3,1,2,0:T(8,128)(2,1)}, u32[]{:S(2)}, u32[]{:S(2)}) %all-to-all-start.3) | async-done | bytes 524320 | tf_op jit(solution)/shard_map/all_to_all | solution.py:21
  128.3 5.5 %all-to-all-start.7 = ((f32[8,128,2,128]{3,1,2,0:T(8,128)}), f32[8,128,2,128]{3,1,2,0:T(8,128)}, u32[]{:S(2)}, u32[]{:S(2)}) async-start(f32[8,128,2,128]{3,1,2,0:T(8,128)} %bitcast.142), calls=%async_computation.7 | async-start | bytes 2097152 | tf_op jit(solution)/shard_map/all_to_all | solution.py:15
  137.1 10.2 %all-to-all-done.7 = f32[8,128,2,128]{3,1,2,0:T(8,128)} async-done(((f32[8,128,2,128]{3,1,2,0:T(8,128)}), f32[8,128,2,128]{3,1,2,0:T(8,128)}, u32[]{:S(2)}, u32[]{:S(2)}) %all-to-all-start.7) | async-done | bytes 1048608 | tf_op jit(solution)/shard_map/all_to_all | solution.py:15
  147.3 5.6 %all-to-all-start.10 = ((f32[8,128,2,128]{3,1,2,0:T(8,128)}), f32[8,128,2,128]{3,1,2,0:T(8,128)}, u32[]{:S(2)}, u32[]{:S(2)}) async-start(f32[8,128,2,128]{3,1,2,0:T(8,128)} %bitcast.141), calls=%async_computation.10 | async-start | bytes 2097152 | tf_op jit(solution)/shard_map/all_to_all | solution.py:15
  156.3 9.6 %all-to-all-done.10 = f32[8,128,2,128]{3,1,2,0:T(8,128)} async-done(((f32[8,128,2,128]{3,1,2,0:T(8,128)}), f32[8,128,2,128]{3,1,2,0:T(8,128)}, u32[]{:S(2)}, u32[]{:S(2)}) %all-to-all-start.10) | async-done | bytes 1048608 | tf_op jit(solution)/shard_map/all_to_all | solution.py:15
  165.9 4.6 all-to-all-start.8
  173.9 6.5 %all-to-all-done.8 = bf16[128,2,128]{2,1,0:T(2,128)(2,1)} async-done(((bf16[128,2,128]{2,1,0:T(2,128)(2,1)}), bf16[128,2,128]{2,1,0:T(2,128)(2,1)}, u32[]{:S(2)}, u32[]{:S(2)}) %all-to-all-start.8) | async-done | bytes 65568 | tf_op jit(solution)/shard_map/all_to_all | solution.py:78
  180.4 4.6 all-to-all-start.11
  186.5 8.4 %all-to-all-done.11 = bf16[128,2,128]{2,1,0:T(2,128)(2,1)} async-done(((bf16[128,2,128]{2,1,0:T(2,128)(2,1)}), bf16[128,2,128]{2,1,0:T(2,128)(2,1)}, u32[]{:S(2)}, u32[]{:S(2)}) %all-to-all-start.11) | async-done | bytes 65568 | tf_op jit(solution)/shard_map/all_to_all | solution.py:78
  196.7 5.5 %all-to-all-start.9 = ((bf16[8,4,64,128]{3,2,1,0:T(8,128)(2,1)}), bf16[8,4,64,128]{3,2,1,0:T(8,128)(2,1)}, u32[]{:S(2)}, u32[]{:S(2)}) async-start(bf16[8,4,64,128]{3,2,1,0:T(8,128)(2,1)} %broadcast_in_dim.26), calls=%async_computation.9 | async-start | bytes 1048576 | tf_op jit(solution)/shard_map/all_to_all | solution.py:21
  211.8 5.5 %all-to-all-start.12 = ((bf16[8,4,64,128]{3,2,1,0:T(8,128)(2,1)}), bf16[8,4,64,128]{3,2,1,0:T(8,128)(2,1)}, u32[]{:S(2)}, u32[]{:S(2)}) async-start(bf16[8,4,64,128]{3,2,1,0:T(8,128)(2,1)} %broadcast_in_dim.28), calls=%async_computation.12 | async-start | bytes 1048576 | tf_op jit(solution)/shard_map/all_to_all | solution.py:21
  225.2 4.7 all-to-all-start.13
  242.2 245.3 %all-reduce.2.cloned.1.call-done = f32[1024,64]{0,1:T(8,128)} async-done(((f32[1024,64]{0,1:T(8,128)}), f32[1024,64]{0,1:T(8,128)}) %all-reduce.2.cloned.1.call-update) | async-done | bytes 262160 | tf_op jit(solution)/shard_map/psum | solution.py:144
  (72 shorter events, 67.4 us)
Async XLA Ops:
  7.2 108.6 %copy-start = (bf16[2,1024,512]{2,1,0:T(8,128)(2,1)S(1)}, bf16[2,1024,512]{2,1,0:T(8,128)(2,1)}, u32[]{:S(2)}) copy-start(bf16[2,1024,512]{2,1,0:T(8,128)(2,1)} %param.8) | copy-start | bytes 6291460
  20.9 199.2 %copy-start.2 = (f32[4,64]{1,0:T(4,128)}, f32[4,64]{1,0:T(4,128)S(1)}, u32[]{:S(2)}) copy-start(f32[4,64]{1,0:T(4,128)S(1)} %get-tuple-element.10) | copy-start | bytes 3076
  20.9 199.2 %copy-start.3 = (f32[4,64]{1,0:T(4,128)}, f32[4,64]{1,0:T(4,128)S(1)}, u32[]{:S(2)}) copy-start(f32[4,64]{1,0:T(4,128)S(1)} %get-tuple-element.11) | copy-start | bytes 3076
  23.4 18.7 %all-to-all-start.4 = ((f32[8,4,64,128]{3,2,1,0:T(8,128)}), f32[8,4,64,128]{3,2,1,0:T(8,128)}, u32[]{:S(2)}, u32[]{:S(2)}) async-start(f32[8,4,64,128]{3,2,1,0:T(8,128)} %bitcast.137), calls=%async_computation.4 | async-start | bytes 2097152 | tf_op jit(solution)/shard_map/all_to_all | solution.py:15
  29.7 12.4 %copy-start.4 = (f32[4,72]{1,0:T(4,128)}, f32[4,72]{1,0:T(4,128)S(1)}, u32[]{:S(2)}) copy-start(f32[4,72]{1,0:T(4,128)S(1)} %get-tuple-element.14) | copy-start | bytes 3460
  42.1 18.0 %all-to-all-start.1 = ((f32[8,4,64,128]{3,2,1,0:T(8,128)}), f32[8,4,64,128]{3,2,1,0:T(8,128)S(1)}, u32[]{:S(2)}, u32[]{:S(2)}) async-start(f32[8,4,64,128]{3,2,1,0:T(8,128)} %bitcast.140), calls=%async_computation.1 | async-start | bytes 2097152 | tf_op jit(solution)/shard_map/all_to_all | solution.py:15
  60.1 21.2 %all-to-all-start.5 = ((bf16[4,64,128]{2,0,1:T(4,128)(2,1)}), bf16[4,64,128]{2,0,1:T(4,128)(2,1)S(1)}, u32[]{:S(2)}, u32[]{:S(2)}) async-start(bf16[4,64,128]{2,0,1:T(4,128)(2,1)} %copy.87), calls=%async_computation.5 | async-start | bytes 131072 | tf_op jit(solution)/shard_map/all_to_all | solution.py:71
  81.2 13.8 %all-to-all-start.2 = ((bf16[4,64,128]{2,0,1:T(4,128)(2,1)}), bf16[4,64,128]{2,0,1:T(4,128)(2,1)S(1)}, u32[]{:S(2)}, u32[]{:S(2)}) async-start(bf16[4,64,128]{2,0,1:T(4,128)(2,1)} %copy.82), calls=%async_computation.2 | async-start | bytes 131072 | tf_op jit(solution)/shard_map/all_to_all | solution.py:71
  95.9 13.5 %all-to-all-start.6 = ((bf16[8,128,2,128]{3,1,2,0:T(8,128)(2,1)}), bf16[8,128,2,128]{3,1,2,0:T(8,128)(2,1)S(1)}, u32[]{:S(2)}, u32[]{:S(2)}) async-start(bf16[8,128,2,128]{3,1,2,0:T(8,128)(2,1)} %broadcast_in_dim.24), calls=%async_computation.6 | async-start | bytes 1048576 | tf_op jit(solution)/shard_map/all_to_all | solution.py:21
  110.3 13.4 %all-to-all-start.3 = ((bf16[8,128,2,128]{3,1,2,0:T(8,128)(2,1)}), bf16[8,128,2,128]{3,1,2,0:T(8,128)(2,1)}, u32[]{:S(2)}, u32[]{:S(2)}) async-start(bf16[8,128,2,128]{3,1,2,0:T(8,128)(2,1)} %broadcast_in_dim.22), calls=%async_computation.3 | async-start | bytes 1048576 | tf_op jit(solution)/shard_map/all_to_all | solution.py:21
  128.3 18.9 %all-to-all-start.7 = ((f32[8,128,2,128]{3,1,2,0:T(8,128)}), f32[8,128,2,128]{3,1,2,0:T(8,128)}, u32[]{:S(2)}, u32[]{:S(2)}) async-start(f32[8,128,2,128]{3,1,2,0:T(8,128)} %bitcast.142), calls=%async_computation.7 | async-start | bytes 2097152 | tf_op jit(solution)/shard_map/all_to_all | solution.py:15
  147.3 18.6 %all-to-all-start.10 = ((f32[8,128,2,128]{3,1,2,0:T(8,128)}), f32[8,128,2,128]{3,1,2,0:T(8,128)}, u32[]{:S(2)}, u32[]{:S(2)}) async-start(f32[8,128,2,128]{3,1,2,0:T(8,128)} %bitcast.141), calls=%async_computation.10 | async-start | bytes 2097152 | tf_op jit(solution)/shard_map/all_to_all | solution.py:15
  165.9 14.5 %all-to-all-start.8 = ((bf16[128,2,128]{2,1,0:T(2,128)(2,1)}), bf16[128,2,128]{2,1,0:T(2,128)(2,1)}, u32[]{:S(2)}, u32[]{:S(2)}) async-start(bf16[128,2,128]{2,1,0:T(2,128)(2,1)} %copy.92), calls=%async_computation.8 | async-start | bytes 131072 | tf_op jit(solution)/shard_map/all_to_all | solution.py:78
  180.4 14.5 %all-to-all-start.11 = ((bf16[128,2,128]{2,1,0:T(2,128)(2,1)}), bf16[128,2,128]{2,1,0:T(2,128)(2,1)}, u32[]{:S(2)}, u32[]{:S(2)}) async-start(bf16[128,2,128]{2,1,0:T(2,128)(2,1)} %copy.97), calls=%async_computation.11 | async-start | bytes 131072 | tf_op jit(solution)/shard_map/all_to_all | solution.py:78
  196.7 14.2 %all-to-all-start.9 = ((bf16[8,4,64,128]{3,2,1,0:T(8,128)(2,1)}), bf16[8,4,64,128]{3,2,1,0:T(8,128)(2,1)}, u32[]{:S(2)}, u32[]{:S(2)}) async-start(bf16[8,4,64,128]{3,2,1,0:T(8,128)(2,1)} %broadcast_in_dim.26), calls=%async_computation.9 | async-start | bytes 1048576 | tf_op jit(solution)/shard_map/all_to_all | solution.py:21
  211.8 13.4 %all-to-all-start.12 = ((bf16[8,4,64,128]{3,2,1,0:T(8,128)(2,1)}), bf16[8,4,64,128]{3,2,1,0:T(8,128)(2,1)}, u32[]{:S(2)}, u32[]{:S(2)}) async-start(bf16[8,4,64,128]{3,2,1,0:T(8,128)(2,1)} %broadcast_in_dim.28), calls=%async_computation.12 | async-start | bytes 1048576 | tf_op jit(solution)/shard_map/all_to_all | solution.py:21
  221.6 18.1 %copy-start.1 = (bf16[1024,64]{0,1:T(8,128)(2,1)S(1)}, bf16[1024,64]{0,1:T(8,128)(2,1)}, u32[]{:S(2)}) copy-start(bf16[1024,64]{0,1:T(8,128)(2,1)} %param.7) | copy-start | bytes 393220
  225.2 9.4 %all-to-all-start.13 = ((f32[8,1,256]{2,1,0:T(1,128)}), f32[8,1,256]{2,1,0:T(1,128)S(1)}, u32[]{:S(2)}, u32[]{:S(2)}) async-start(f32[8,1,256]{2,1,0:T(1,128)} %reshape.65), calls=%async_computation.13 | async-start | bytes 16384 | tf_op jit(solution)/shard_map/all_to_all | solution.py:21
  229.9 257.6 %all-reduce.2.cloned.1.call-start = ((), (), s32[]{:S(2)}) async-start(), calls=%async_computation.14 | async-start | bytes 524288 | tf_op jit(solution)/shard_map/psum | solution.py:144
Sparse Core Ops, SparseCore 0:
  239.8 247.6 all-reduce.1
where the time goes:
time: 498 us; the launch traced here: 496 us
  waiting for transfers between devices  345 us (69%)
  starting transfers between devices  71.8 us (14%)
  matrix products  26.7 us (5%)
  local copies, waits for them, and re-layouts  19.7 us (4%)
  between operations  14.3 us (3%)
  blocking collectives  10.4 us (2%)
  other arithmetic  8.52 us (2%)
    psum x1, waiting for transfers between devices, on_device(): grad_router = lax.psum(local_router, ('dp', 'tensor'))  245 us
    all_to_all x4, waiting for transfers between devices, summed_on_arrival(): lax.all_to_all(blocks, axis, split_axis=0, concat_axis=0, tiled=True)  40.8 us
    all_to_all x5, starting transfers between devices, sent_to_all(): lax.all_to_all(jnp.broadcast_to(x[None], (length, *x.shape)), axis, 0, 0,...  26 us
    all_to_all x5, waiting for transfers between devices, sent_to_all(): lax.all_to_all(jnp.broadcast_to(x[None], (length, *x.shape)), axis, 0, 0,...  24.6 us
    all_to_all x4, starting transfers between devices, summed_on_arrival(): lax.all_to_all(blocks, axis, split_axis=0, concat_axis=0, tiled=True)  21.6 us
    all_to_all x2, waiting for transfers between devices, to_experts(): lax.all_to_all(shared_part, 'dp', split_axis=1, concat_axis=0, tiled=True)  19.1 us
    all_to_all x2, starting transfers between devices, to_experts(): lax.all_to_all(shared_part, 'dp', split_axis=1, concat_axis=0, tiled=True)  15.1 us
    all_to_all x2, waiting for transfers between devices, to_images(): lax.all_to_all(shared_part, 'dp', split_axis=0, concat_axis=1, tiled=True)  14.8 us
  transfers between devices with their start and end apart: 14, of which 14 were waited for; matrix products, arithmetic and copies ran while one was open for 7% of the time, Pallas kernels for 0%

commit v1 on v0

--- a/solution.py
+++ b/solution.py
@@ -141,7 +141,7 @@
     )
     grad_tokens = (token_part + router_part).astype(jnp.bfloat16)
     local_router = jnp.einsum("isd,ise->de", tokens, grad_logits, preferred_element_type=wide)
-    grad_router = lax.psum(local_router, ("dp", "tensor"))
+    grad_router = lax.psum(lax.psum(local_router, "dp"), "tensor")
     return (grad_tokens, grad_router, grad_w_in, grad_w_out)
 
 

time: 498 us -> 590 us (1.18)
  waiting for transfers between devices: 345 us -> 446 us
    psum x1 -> x2, waiting for transfers between devices: 245 us -> 339 us  [on_device(): grad_router = lax.psum(lax.psum(local_router, 'dp'), 'tensor')]
  transfers between devices with their start and end apart: 14 -> 15, of which waited for: 14 -> 15; matrix products, arithmetic and copies ran while one was open for 7% -> 5% of each run, Pallas kernels for 0% -> 0%
where the time goes in v1:
time: 590 us; the launch traced here: 587 us
  waiting for transfers between devices  446 us (76%)
  starting transfers between devices  70.5 us (12%)
  matrix products  25.8 us (4%)
  between operations  14.3 us (2%)
  local copies, waits for them, and re-layouts  14.2 us (2%)
  blocking collectives  10.4 us (2%)
  other arithmetic  6.26 us (1%)
    psum x2, waiting for transfers between devices, on_device(): grad_router = lax.psum(lax.psum(local_router, 'dp'), 'tensor')  339 us
    all_to_all x4, waiting for transfers between devices, summed_on_arrival(): lax.all_to_all(blocks, axis, split_axis=0, concat_axis=0, tiled=True)  42.3 us
    all_to_all x5, waiting for transfers between devices, sent_to_all(): lax.all_to_all(jnp.broadcast_to(x[None], (length, *x.shape)), axis, 0, 0,...  27.4 us
    all_to_all x5, starting transfers between devices, sent_to_all(): lax.all_to_all(jnp.broadcast_to(x[None], (length, *x.shape)), axis, 0, 0,...  26.1 us
    all_to_all x4, starting transfers between devices, summed_on_arrival(): lax.all_to_all(blocks, axis, split_axis=0, concat_axis=0, tiled=True)  21.5 us
    all_to_all x2, waiting for transfers between devices, to_experts(): lax.all_to_all(shared_part, 'dp', split_axis=1, concat_axis=0, tiled=True)  19.1 us
    all_to_all x2, waiting for transfers between devices, to_images(): lax.all_to_all(shared_part, 'dp', split_axis=0, concat_axis=1, tiled=True)  17.8 us
    all_to_all x2, starting transfers between devices, to_experts(): lax.all_to_all(shared_part, 'dp', split_axis=1, concat_axis=0, tiled=True)  15.1 us
  transfers between devices with their start and end apart: 15, of which 15 were waited for; matrix products, arithmetic and copies ran while one was open for 5% of the time, Pallas kernels for 0%

profile of v1, /device:TPU:2, one launch (start us, length us, event | category | flops | bytes accessed | tf_op | source)
XLA Modules:
  0.0 587.4 jit_solution(12457951196065443920)
XLA Ops:
  9.2 10.4 %all_to_all.110 = f32[8,1,512]{2,1,0:T(1,128)S(1)} all-to-all(f32[8,1,512]{2,1,0:T(1,128)S(1)} %reshape.63), channel_id=1, replica_groups=mesh['dp'=32,'tensor'=8] {'tensor'}, dimensions={0} | all-to-all | bytes 32768 | tf_op jit(solution)/shard_map/all_to_all | solution.py:21
  23.5 5.6 all-to-all-start.4
  32.3 9.9 %all-to-all-done.4 = f32[8,4,64,128]{3,2,1,0:T(8,128)} async-done(((f32[8,4,64,128]{3,2,1,0:T(8,128)}), f32[8,4,64,128]{3,2,1,0:T(8,128)}, u32[]{:S(2)}, u32[]{:S(2)}) %all-to-all-start.4) | async-done | bytes 1048608 | tf_op jit(solution)/shard_map/all_to_all | solution.py:15
  42.2 4.9 all-to-all-start.1
  49.1 11.1 %all-to-all-done.1 = f32[8,4,64,128]{3,2,1,0:T(8,128)S(1)} async-done(((f32[8,4,64,128]{3,2,1,0:T(8,128)}), f32[8,4,64,128]{3,2,1,0:T(8,128)S(1)}, u32[]{:S(2)}, u32[]{:S(2)}) %all-to-all-start.1) | async-done | bytes 1048608 | tf_op jit(solution)/shard_map/all_to_all | solution.py:15
  60.2 11.2 %all-to-all-start.5 = ((bf16[4,64,128]{2,0,1:T(4,128)(2,1)}), bf16[4,64,128]{2,0,1:T(4,128)(2,1)S(1)}, u32[]{:S(2)}, u32[]{:S(2)}) async-start(bf16[4,64,128]{2,0,1:T(4,128)(2,1)} %copy.87), calls=%async_computation.5 | async-start | bytes 131072 | tf_op jit(solution)/shard_map/all_to_all | solution.py:71
  72.2 9.2 %all-to-all-done.5 = bf16[4,64,128]{2,0,1:T(4,128)(2,1)S(1)} async-done(((bf16[4,64,128]{2,0,1:T(4,128)(2,1)}), bf16[4,64,128]{2,0,1:T(4,128)(2,1)S(1)}, u32[]{:S(2)}, u32[]{:S(2)}) %all-to-all-start.5) | async-done | bytes 65568 | tf_op jit(solution)/shard_map/all_to_all | solution.py:71
  85.3 9.9 %all-to-all-done.2 = bf16[4,64,128]{2,0,1:T(4,128)(2,1)S(1)} async-done(((bf16[4,64,128]{2,0,1:T(4,128)(2,1)}), bf16[4,64,128]{2,0,1:T(4,128)(2,1)S(1)}, u32[]{:S(2)}, u32[]{:S(2)}) %all-to-all-start.2) | async-done | bytes 65568 | tf_op jit(solution)/shard_map/all_to_all | solution.py:71
  96.1 4.9 all-to-all-start.6
  101.0 8.5 %all-to-all-done.6 = bf16[8,128,2,128]{3,1,2,0:T(8,128)(2,1)S(1)} async-done(((bf16[8,128,2,128]{3,1,2,0:T(8,128)(2,1)}), bf16[8,128,2,128]{3,1,2,0:T(8,128)(2,1)S(1)}, u32[]{:S(2)}, u32[]{:S(2)}) %all-to-all-start.6) | async-done | bytes 524320 | tf_op jit(solution)/shard_map/all_to_all | solution.py:21
  110.4 5.5 all-to-all-start.3
  116.4 7.5 %all-to-all-done.3 = bf16[8,128,2,128]{3,1,2,0:T(8,128)(2,1)} async-done(((bf16[8,128,2,128]{3,1,2,0:T(8,128)(2,1)}), bf16[8,128,2,128]{3,1,2,0:T(8,128)(2,1)}, u32[]{:S(2)}, u32[]{:S(2)}) %all-to-all-start.3) | async-done | bytes 524320 | tf_op jit(solution)/shard_map/all_to_all | solution.py:21
  128.5 5.5 all-to-all-start.7
  137.2 10.2 %all-to-all-done.7 = f32[8,128,2,128]{3,1,2,0:T(8,128)} async-done(((f32[8,128,2,128]{3,1,2,0:T(8,128)}), f32[8,128,2,128]{3,1,2,0:T(8,128)}, u32[]{:S(2)}, u32[]{:S(2)}) %all-to-all-start.7) | async-done | bytes 1048608 | tf_op jit(solution)/shard_map/all_to_all | solution.py:15
  147.4 5.6 all-to-all-start.10
  155.0 11.1 %all-to-all-done.10 = f32[8,128,2,128]{3,1,2,0:T(8,128)} async-done(((f32[8,128,2,128]{3,1,2,0:T(8,128)}), f32[8,128,2,128]{3,1,2,0:T(8,128)}, u32[]{:S(2)}, u32[]{:S(2)}) %all-to-all-start.10) | async-done | bytes 1048608 | tf_op jit(solution)/shard_map/all_to_all | solution.py:15
  171.9 8.0 %all-to-all-done.8 = bf16[128,2,128]{2,1,0:T(2,128)(2,1)S(1)} async-done(((bf16[128,2,128]{2,1,0:T(2,128)(2,1)}), bf16[128,2,128]{2,1,0:T(2,128)(2,1)S(1)}, u32[]{:S(2)}, u32[]{:S(2)}) %all-to-all-start.8) | async-done | bytes 65568 | tf_op jit(solution)/shard_map/all_to_all | solution.py:78
  183.8 9.9 %all-to-all-done.11 = bf16[128,2,128]{2,1,0:T(2,128)(2,1)S(1)} async-done(((bf16[128,2,128]{2,1,0:T(2,128)(2,1)}), bf16[128,2,128]{2,1,0:T(2,128)(2,1)S(1)}, u32[]{:S(2)}, u32[]{:S(2)}) %all-to-all-start.11) | async-done | bytes 65568 | tf_op jit(solution)/shard_map/all_to_all | solution.py:78
  194.6 5.5 all-to-all-start.9
  203.3 5.5 all-to-all-done.9
  209.7 5.6 all-to-all-start.12
  223.2 4.7 all-to-all-start.13
  237.1 262.0 %all-reduce.3.cloned.1.call-done = f32[1024,64]{0,1:T(8,128)} async-done(((f32[1024,64]{0,1:T(8,128)}), f32[1024,64]{0,1:T(8,128)}) %all-reduce.3.cloned.1.call-update) | async-done | bytes 262160 | tf_op jit(solution)/shard_map/psum | solution.py:144
  501.7 77.2 %all-reduce.5.cloned.1.call-done = f32[1024,64]{0,1:T(8,128)} async-done(((f32[1024,64]{0,1:T(8,128)}), f32[1024,64]{0,1:T(8,128)}) %all-reduce.5.cloned.1.call-update) | async-done | bytes 262160 | tf_op jit(solution)/shard_map/psum | solution.py:144
  (77 shorter events, 63.9 us)
Async XLA Ops:
  7.2 108.8 %copy-start = (bf16[2,1024,512]{2,1,0:T(8,128)(2,1)S(1)}, bf16[2,1024,512]{2,1,0:T(8,128)(2,1)}, u32[]{:S(2)}) copy-start(bf16[2,1024,512]{2,1,0:T(8,128)(2,1)} %param.8) | copy-start | bytes 6291460
  23.5 18.7 %all-to-all-start.4 = ((f32[8,4,64,128]{3,2,1,0:T(8,128)}), f32[8,4,64,128]{3,2,1,0:T(8,128)}, u32[]{:S(2)}, u32[]{:S(2)}) async-start(f32[8,4,64,128]{3,2,1,0:T(8,128)} %bitcast.137), calls=%async_computation.4 | async-start | bytes 2097152 | tf_op jit(solution)/shard_map/all_to_all | solution.py:15
  42.2 18.0 %all-to-all-start.1 = ((f32[8,4,64,128]{3,2,1,0:T(8,128)}), f32[8,4,64,128]{3,2,1,0:T(8,128)S(1)}, u32[]{:S(2)}, u32[]{:S(2)}) async-start(f32[8,4,64,128]{3,2,1,0:T(8,128)} %bitcast.140), calls=%async_computation.1 | async-start | bytes 2097152 | tf_op jit(solution)/shard_map/all_to_all | solution.py:15
  60.2 21.2 %all-to-all-start.5 = ((bf16[4,64,128]{2,0,1:T(4,128)(2,1)}), bf16[4,64,128]{2,0,1:T(4,128)(2,1)S(1)}, u32[]{:S(2)}, u32[]{:S(2)}) async-start(bf16[4,64,128]{2,0,1:T(4,128)(2,1)} %copy.87), calls=%async_computation.5 | async-start | bytes 131072 | tf_op jit(solution)/shard_map/all_to_all | solution.py:71
  81.4 13.8 %all-to-all-start.2 = ((bf16[4,64,128]{2,0,1:T(4,128)(2,1)}), bf16[4,64,128]{2,0,1:T(4,128)(2,1)S(1)}, u32[]{:S(2)}, u32[]{:S(2)}) async-start(bf16[4,64,128]{2,0,1:T(4,128)(2,1)} %copy.82), calls=%async_computation.2 | async-start | bytes 131072 | tf_op jit(solution)/shard_map/all_to_all | solution.py:71
  96.1 13.5 %all-to-all-start.6 = ((bf16[8,128,2,128]{3,1,2,0:T(8,128)(2,1)}), bf16[8,128,2,128]{3,1,2,0:T(8,128)(2,1)S(1)}, u32[]{:S(2)}, u32[]{:S(2)}) async-start(bf16[8,128,2,128]{3,1,2,0:T(8,128)(2,1)} %broadcast_in_dim.24), calls=%async_computation.6 | async-start | bytes 1048576 | tf_op jit(solution)/shard_map/all_to_all | solution.py:21
  110.4 13.4 %all-to-all-start.3 = ((bf16[8,128,2,128]{3,1,2,0:T(8,128)(2,1)}), bf16[8,128,2,128]{3,1,2,0:T(8,128)(2,1)}, u32[]{:S(2)}, u32[]{:S(2)}) async-start(bf16[8,128,2,128]{3,1,2,0:T(8,128)(2,1)} %broadcast_in_dim.22), calls=%async_computation.3 | async-start | bytes 1048576 | tf_op jit(solution)/shard_map/all_to_all | solution.py:21
  126.6 1.9 copy-start.2
  128.5 18.9 %all-to-all-start.7 = ((f32[8,128,2,128]{3,1,2,0:T(8,128)}), f32[8,128,2,128]{3,1,2,0:T(8,128)}, u32[]{:S(2)}, u32[]{:S(2)}) async-start(f32[8,128,2,128]{3,1,2,0:T(8,128)} %bitcast.142), calls=%async_computation.7 | async-start | bytes 2097152 | tf_op jit(solution)/shard_map/all_to_all | solution.py:15
  147.4 18.6 %all-to-all-start.10 = ((f32[8,128,2,128]{3,1,2,0:T(8,128)}), f32[8,128,2,128]{3,1,2,0:T(8,128)}, u32[]{:S(2)}, u32[]{:S(2)}) async-start(f32[8,128,2,128]{3,1,2,0:T(8,128)} %bitcast.141), calls=%async_computation.10 | async-start | bytes 2097152 | tf_op jit(solution)/shard_map/all_to_all | solution.py:15
  166.0 13.8 %all-to-all-start.8 = ((bf16[128,2,128]{2,1,0:T(2,128)(2,1)}), bf16[128,2,128]{2,1,0:T(2,128)(2,1)S(1)}, u32[]{:S(2)}, u32[]{:S(2)}) async-start(bf16[128,2,128]{2,1,0:T(2,128)(2,1)} %copy.92), calls=%async_computation.8 | async-start | bytes 131072 | tf_op jit(solution)/shard_map/all_to_all | solution.py:78
  179.8 13.8 %all-to-all-start.11 = ((bf16[128,2,128]{2,1,0:T(2,128)(2,1)}), bf16[128,2,128]{2,1,0:T(2,128)(2,1)S(1)}, u32[]{:S(2)}, u32[]{:S(2)}) async-start(bf16[128,2,128]{2,1,0:T(2,128)(2,1)} %copy.97), calls=%async_computation.11 | async-start | bytes 131072 | tf_op jit(solution)/shard_map/all_to_all | solution.py:78
  194.6 14.2 %all-to-all-start.9 = ((bf16[8,4,64,128]{3,2,1,0:T(8,128)(2,1)}), bf16[8,4,64,128]{3,2,1,0:T(8,128)(2,1)}, u32[]{:S(2)}, u32[]{:S(2)}) async-start(bf16[8,4,64,128]{3,2,1,0:T(8,128)(2,1)} %broadcast_in_dim.26), calls=%async_computation.9 | async-start | bytes 1048576 | tf_op jit(solution)/shard_map/all_to_all | solution.py:21
  209.7 8.6 %copy-start.1 = (bf16[4,72,1024]{2,1,0:T(8,128)(2,1)S(1)}, bf16[4,72,1024]{2,1,0:T(8,128)(2,1)}, u32[]{:S(2)}) copy-start(bf16[4,72,1024]{2,1,0:T(8,128)(2,1)} %param.5) | copy-start | bytes 1769476
  209.7 13.5 %all-to-all-start.12 = ((bf16[8,4,64,128]{3,2,1,0:T(8,128)(2,1)}), bf16[8,4,64,128]{3,2,1,0:T(8,128)(2,1)}, u32[]{:S(2)}, u32[]{:S(2)}) async-start(bf16[8,4,64,128]{3,2,1,0:T(8,128)(2,1)} %broadcast_in_dim.28), calls=%async_computation.12 | async-start | bytes 1048576 | tf_op jit(solution)/shard_map/all_to_all | solution.py:21
  219.7 15.8 %copy-start.4 = (f32[4,72,64]{1,2,0:T(8,128)}, f32[4,72,64]{1,2,0:T(8,128)S(1)}, u32[]{:S(2)}) copy-start(f32[4,72,64]{1,2,0:T(8,128)S(1)} %get-tuple-element.17) | copy-start | bytes 221188
  223.2 9.4 %all-to-all-start.13 = ((f32[8,1,256]{2,1,0:T(1,128)}), f32[8,1,256]{2,1,0:T(1,128)S(1)}, u32[]{:S(2)}, u32[]{:S(2)}) async-start(f32[8,1,256]{2,1,0:T(1,128)} %reshape.65), calls=%async_computation.13 | async-start | bytes 16384 | tf_op jit(solution)/shard_map/all_to_all | solution.py:21
  227.9 271.3 %all-reduce.3.cloned.1.call-start = ((), (), s32[]{:S(2)}) async-start(), calls=%async_computation.14 | async-start | bytes 524288 | tf_op jit(solution)/shard_map/psum | solution.py:144
  229.4 6.1 %copy-start.5 = (f32[4,72,64]{1,2,0:T(8,128)}, f32[4,72,64]{1,2,0:T(8,128)S(1)}, u32[]{:S(2)}) copy-start(f32[4,72,64]{1,2,0:T(8,128)S(1)} %convolution_bitcast_fusion.8) | copy-start | bytes 221188
  229.5 269.8 %copy-start.3 = (bf16[1024,64]{0,1:T(8,128)(2,1)S(1)}, bf16[1024,64]{0,1:T(8,128)(2,1)}, u32[]{:S(2)}) copy-start(bf16[1024,64]{0,1:T(8,128)(2,1)} %param.7) | copy-start | bytes 393220
  235.6 343.3 %all-reduce.5.cloned.1.call-start = ((), (), s32[]{:S(2)}) async-start(), calls=%async_computation.15 | async-start | bytes 524288 | tf_op jit(solution)/shard_map/psum | solution.py:144
Sparse Core Ops, SparseCore 0:
  235.7 263.4 all-reduce.2
  501.8 77.0 all-reduce.4
